TPU v7x, 256 devices: a whole 4x4x8 slice. The times are simulated.
256 devices in a mesh: row: 32 (over y, x, core), col: 8 (over z).
Axes of the slice: x: 4, y: 4, z: 8, core: 2. Of those that a mesh axis runs over, the one named last changes fastest.
Arguments:
- vectors: float32 [16384, 16384], P('row', 'col'), may hold values from -0.046875 to 0.046875
- basis: float32 [16384, 2048], P('col', 'row'), may hold values from -9 to 9
- block_units: int32 [8], replicated, may hold values from 1 to 40, 64 in all
Outputs:
- assembled: float32 [16384, 2048], P('row', 'col')
Inputs may be any that keep to these rules, and one draw needn't show every extreme that they name: `block_units`: the block sizes are whole numbers of units that sum to 64; the largest is exactly the maximum.
All inputs are finite; a program needn't handle non-finite values.
Results may differ from a plain program's by a relative error of at most 0.00007.
Values sent between devices are 32-bit elements; how exact they have to be, the bound alone decides.
A program may use at most 64 MiB of HBM per device.

v0:
```python
import jax.numpy as jnp
from jax import lax

N = 16384
W = 2048
UNIT = 256
START = 7168


def block_ids(positions, block_units):
    ends = jnp.cumsum(block_units).astype(jnp.int32) * UNIT
    return jnp.sum((positions[:, None] >= ends[None, :-1]).astype(jnp.int32), axis=1)


def reference(vectors, basis, block_units):
    row_block = block_ids(jnp.arange(N, dtype=jnp.int32), block_units)
    slab_block = block_ids(START + jnp.arange(W, dtype=jnp.int32), block_units)
    masked = jnp.where(row_block[:, None] == slab_block[None, :], basis, jnp.float32(0.0))
    return jnp.dot(
        vectors, masked, precision=lax.Precision.HIGHEST, preferred_element_type=jnp.float32
    )


def solution(mesh):
    return reference
```

profile of v0, /device:TPU:32, one launch (start us, length us, event | category | flops | bytes accessed | tf_op | source)
XLA Modules:
  0.0 187.8 jit_solution(9073849661509887973)
XLA Ops:
  6.5 0.0 all-gather.3.cloned.1.call-start
  6.5 1.3 dynamic-slice.1
  8.5 1.3 dynamic-slice
  9.7 0.8 reduce-window.8
  11.2 0.1 convert_reduce_fusion.1
  11.3 0.1 convert_reduce_fusion
  11.4 1.9 %compare_select_fusion = f32[2048,64]{0,1:T(8,128)} fusion(f32[2048,64]{0,1:T(8,128)} %param.1, s32[2048]{0:T(1024)S(1)} %convert_reduce_fusion, s32[64]{0:T(128)S(1)} %convert_reduce_fusion.1), kind=kLoop, calls=%fused_computation | loop fusion | flops 262144 | bytes 1057024 | tf_op jit(solution)/jit(_where)/select_n | solution.py:18
  13.3 0.0 all-gather.3.cloned.1.call-update
  13.4 0.0 reduce-scatter.4.cloned.1.call-start
  13.4 80.3 %all-gather.3.cloned.1.call-done = f32[2048,2048]{0,1:T(8,128)} async-done(((f32[2048,64]{0,1:T(8,128)}), f32[2048,2048]{0,1:T(8,128)}) %all-gather.3.cloned.1.call-update) | async-done | bytes 16777232 | tf_op jit(solution)/jit(_where)/select_n | solution.py:18
  93.7 31.9 %fusion = f32[2048,512]{1,0:T(8,128)} fusion(f32[2048,2048]{0,1:T(8,128)} %all-gather.3.cloned.1.call-done, f32[512,2048]{1,0:T(8,128)} %param.2), kind=kOutput, calls=%fused_computation.7 | convolution fusion | flops 25769803776 | bytes 25165824 | tf_op jit(solution)/dot_general | solution.py:19
  125.6 0.0 reduce-scatter.4.cloned.1.call-update
  125.6 53.3 %reduce-scatter.4.cloned.1.call-done = f32[256,512]{1,0:T(8,128)} async-done(((f32[2048,512]{1,0:T(8,128)}), f32[256,512]{1,0:T(8,128)}) %reduce-scatter.4.cloned.1.call-update) | async-done | bytes 524304
  178.9 2.0 %copy.1 = f32[512,256]{1,0:T(8,128)} copy(f32[512,256]{0,1:T(8,128)} %bitcast.9) | data formatting | bytes 1048576 | tf_op jit(solution)/dot_general | solution.py:19
  (3 shorter events, 0.0 us)
Async XLA Ops:
  6.5 87.1 %all-gather.3.cloned.1.call-start = ((), (), s32[]{:S(2)}) async-start(), calls=%async_computation.1 | async-start | bytes 17301504 | tf_op jit(solution)/jit(_where)/select_n | solution.py:18
  13.4 165.5 %reduce-scatter.4.cloned.1.call-start = ((), (), s32[]{:S(2)}) async-start(), calls=%async_computation.2 | async-start | bytes 4718592
Sparse Core Ops, SparseCore 0:
  13.5 80.1 all-gather.2
  125.7 53.1 reduce-scatter.3
where the time goes:
time: 191 us; the launch traced here: 188 us
  waiting for transfers between devices  134 us (70%)
  matrix products  31.9 us (17%)
  between operations  14.7 us (8%)
  local copies, waits for them, and re-layouts  4.57 us (2%)
  other arithmetic  2.96 us (2%)
    select_n x1, waiting for transfers between devices, reference(): jnp.where(row_block[:, None] == slab_block[None, :], basis, jnp.float32(0...  80.3 us
    unnamed x3, waiting for transfers between devices  53.3 us
    dot_general x1, matrix products, reference(): jnp.dot(vectors, masked, precision=lax.Precision.HIGHEST, preferred_eleme...  31.9 us
  transfers between devices with their start and end apart: 2, of which 2 were waited for; matrix products, arithmetic and copies ran while one was open for 0% of the time, Pallas kernels for 0%

commit v1 on v0

v1 whole, which is shorter than its diff:
```python
import functools

import jax
import jax.numpy as jnp
from jax import lax
from jax.experimental import pallas as pl
from jax.experimental.pallas import tpu as pltpu
from jax.sharding import PartitionSpec as P

MESH = pl.DeviceIdType.MESH
UNIT = 256
START = 7168
RINGS = 4
PHASES = 8


def kernel(dims, units_ref, v_hbm, bt_hbm, o_ref, gathered, v_mem, weights, lhs, part, up_first, up_rest, down_first,
           down_rest, local_sem, own_sem, gather_sem, gather_sent, mate_sem, mate_sent, sum_sem, sum_sent):
    rows, depth, own, devices, planes = dims
    step = own // PHASES
    width = step * devices
    half = depth // 2
    chunk = width // planes
    per_keep = own * devices // planes // own

    me = lax.axis_index("row")
    z = lax.axis_index("col")
    core = lax.rem(me, 2)
    x = lax.rem(lax.div(me, 2), RINGS)
    y = lax.div(me, 2 * RINGS)

    def at(xx, yy):
        return (yy * RINGS + xx) * 2 + core

    def shift(c, by, n):
        return lax.rem(c + (by % n), n)

    mate = me + 1 - 2 * core
    neighbour = {
        ("x", 1): (at(shift(x, 1, RINGS), y), z),
        ("x", -1): (at(shift(x, -1, RINGS), y), z),
        ("y", 1): (at(x, shift(y, 1, RINGS)), z),
        ("y", -1): (at(x, shift(y, -1, RINGS)), z),
    }
    mate_id = (mate, z)
    up_id = (me, shift(z, 1, planes))
    down_id = (me, shift(z, -1, planes))
    axes = (("x", "y"), ("y", "x"))

    load_v = pltpu.make_async_copy(v_hbm, v_mem, local_sem)
    load_v.start()
    for q in range(PHASES):
        pltpu.make_async_copy(
            bt_hbm.at[pl.ds(q * step, step)],
            gathered.at[q, pl.ds(pl.multiple_of(me * step, step), step)],
            own_sem.at[q],
        ).start()

    barrier = pltpu.get_barrier_semaphore()
    for other in (*neighbour.values(), mate_id, up_id, down_id):
        pl.semaphore_signal(barrier, inc=1, device_id=other, device_id_type=MESH)
    pl.semaphore_wait(barrier, 7)

    def piece(q, h, fo, so):
        if h == 0:
            source = at(shift(x, fo, RINGS), shift(y, so, RINGS))
        else:
            source = at(shift(x, so, RINGS), shift(y, fo, RINGS))
        return gathered.at[q, pl.ds(pl.multiple_of(source * step, step), step), pl.ds(h * half, half)]

    def send(q, h, fo, so, which, direction):
        ref = piece(q, h, fo, so)
        nfo, nso = (fo - direction, so) if which == 0 else (fo, so - direction)
        pltpu.make_async_remote_copy(
            src_ref=ref,
            dst_ref=ref,
            send_sem=gather_sent.at[q],
            recv_sem=gather_sem.at[q, h, (nfo % RINGS) * RINGS + nso % RINGS],
            device_id=neighbour[axes[h][which], direction],
            device_id_type=MESH,
        ).start()

    def arrived(q, h, fo, so):
        ref = piece(q, h, fo, so)
        pltpu.make_async_copy(ref, ref, gather_sem.at[q, h, (fo % RINGS) * RINGS + so % RINGS]).wait()

    def share(q, h, fo, so):
        ref = piece(q, h, fo, so)
        pltpu.make_async_remote_copy(
            src_ref=ref, dst_ref=ref, send_sem=mate_sent.at[q], recv_sem=mate_sem.at[q], device_id=mate_id, device_id_type=MESH
        ).start()

    def first_way(q, h):
        return 1 if (q + h) % 2 == 0 else -1

    def second_way(q, h, fo):
        return 1 if (q + fo // 2 + fo) % 2 == 0 else -1

    def level0(q):
        pltpu.make_async_copy(
            bt_hbm.at[pl.ds(q * step, step)],
            gathered.at[q, pl.ds(pl.multiple_of(me * step, step), step)],
            own_sem.at[q],
        ).wait()
        for h in range(2):
            for direction in (1, -1):
                send(q, h, 0, 0, 0, direction)
        for h in range(2):
            for direction in (1, -1):
                send(q, h, 0, 0, 1, direction)
        for h in range(2):
            share(q, h, 0, 0)

    def along_second(q, h, fo):
        for direction in (1, -1):
            send(q, h, fo, 0, 1, direction)
        share(q, h, fo, 0)

    def level1(q):
        for fo in (-1, 1):
            for h in range(2):
                arrived(q, h, fo, 0)
                if first_way(q, h) == -fo:
                    send(q, h, fo, 0, 0, -fo)
                along_second(q, h, fo)

    def cross(q, h, fo):
        for so in (-1, 1):
            arrived(q, h, fo, so)
            if second_way(q, h, fo) == -so:
                send(q, h, fo, so, 1, -so)
            share(q, h, fo, so)

    def level2(q):
        for h in range(2):
            cross(q, h, 0)
        for h in range(2):
            arrived(q, h, 2, 0)
            along_second(q, h, 2)

    def level3(q):
        for fo in (-1, 1, 2):
            for h in range(2):
                cross(q, h, fo)

    def level4(q):
        for fo in (0, -1, 1, 2):
            for h in range(2):
                arrived(q, h, fo, 2)
                share(q, h, fo, 2)

    def prepare():
        load_v.wait()
        tile = 256

        def body(t, _):
            at_k = pl.multiple_of(t * tile, tile)
            block = v_mem[:, pl.ds(at_k, tile)].T
            hi = block.astype(jnp.bfloat16)
            lo = (block - hi.astype(jnp.float32)).astype(jnp.bfloat16)
            weights[pl.ds(at_k, tile), :] = hi
            weights[pl.ds(pl.multiple_of(depth + at_k, tile), tile), :] = lo
            weights[pl.ds(pl.multiple_of(2 * depth + at_k, tile), tile), :] = hi
            return 0

        lax.fori_loop(0, depth // tile, body, 0)

    ends = []
    total = 0
    for b in range(7):
        total = total + units_ref[b] * UNIT
        ends.append(total)

    def block_of(position):
        ids = jnp.zeros_like(position)
        for end in ends:
            ids = ids + (position >= end).astype(jnp.int32)
        return ids

    def multiply(q):
        group = 16
        row_block = block_of(z * depth + lax.broadcasted_iota(jnp.int32, (1, depth), 1))

        def split(g, _):
            first = pl.multiple_of(g * group, group)
            index = first + lax.broadcasted_iota(jnp.int32, (group, 1), 0)
            column = lax.div(index, step) * own + q * step + lax.rem(index, step)
            keep = block_of(START + column) == row_block
            block = jnp.where(keep, gathered[q, pl.ds(first, group), :], 0.0)
            hi = block.astype(jnp.bfloat16)
            lo = (block - hi.astype(jnp.float32)).astype(jnp.bfloat16)
            lhs[pl.ds(first, group), 0:depth] = hi
            lhs[pl.ds(first, group), depth:2 * depth] = hi
            lhs[pl.ds(first, group), 2 * depth:3 * depth] = lo
            return 0

        lax.fori_loop(0, width // group, split, 0)
        part[q] = jnp.dot(lhs[...], weights[...], preferred_element_type=jnp.float32)

    def chunk_rows(plane, start=0, size=chunk):
        return pl.ds(pl.multiple_of(plane * chunk + start, 8), size)

    def sum_copy(q, s, direction):
        if s == 1:
            start = 0 if direction == 1 else chunk // 2
            src = part.at[q, chunk_rows(shift(z, 4, planes), start, chunk // 2)]
            dst = (up_first if direction == 1 else down_first).at[q]
        else:
            src = part.at[q, chunk_rows(shift(z, direction * (5 - s), planes))]
            dst = (up_rest if direction == 1 else down_rest).at[q, s - 2]
        lane = 0 if direction == 1 else 1
        return pltpu.make_async_remote_copy(
            src_ref=src,
            dst_ref=dst,
            send_sem=sum_sent.at[q, lane, s - 1],
            recv_sem=sum_sem.at[q, lane, s - 1],
            device_id=up_id if direction == 1 else down_id,
            device_id_type=MESH,
        )

    def sum_first(q):
        for direction in (1, -1):
            sum_copy(q, 1, direction).start()

    def sum_next(q, s):
        for direction in (1, -1):
            sum_copy(q, s - 1, direction).wait_recv()
            got = up_first if direction == 1 else down_first
            target = shift(z, direction * (5 - s), planes)
            if s == 2:
                start = 0 if direction == 1 else chunk // 2
                where = chunk_rows(target, start, chunk // 2)
                part[q, where, :] = part[q, where, :] + got[q]
            else:
                got = up_rest if direction == 1 else down_rest
                where = chunk_rows(target)
                part[q, where, :] = part[q, where, :] + got[q, s - 3]
            sum_copy(q, s, direction).start()

    def sum_last(q):
        for direction in (1, -1):
            sum_copy(q, 4, direction).wait_recv()
        total = part[q, chunk_rows(z), :] + up_rest[q, 2] + down_rest[q, 2]
        for i in range(per_keep):
            o_ref[i * own + q * step:i * own + (q + 1) * step, :] = total[i * step:(i + 1) * step, :]

    def sums(q, s):
        if 0 <= q < PHASES:
            if s == 1:
                sum_first(q)
            elif s == 5:
                sum_last(q)
            else:
                sum_next(q, s)

    def drain(q):
        n = 2 * (RINGS * RINGS - 1)
        ref = gathered.at[q, pl.ds(0, n // 2 * step)]
        pltpu.make_async_copy(ref, ref, gather_sent.at[q]).wait()
        ref = gathered.at[q, pl.ds(0, RINGS * RINGS * step)]
        pltpu.make_async_copy(ref, ref, mate_sent.at[q]).wait()
        for s in range(1, 5):
            for direction in (1, -1):
                sum_copy(q, s, direction).wait_send()

    def mate_arrived(q):
        ref = gathered.at[q, pl.ds(0, RINGS * RINGS * step)]
        pltpu.make_async_copy(ref, ref, mate_sem.at[q]).wait()

    level0(0)
    level0(1)
    prepare()
    level1(0)
    for q in range(PHASES):
        level2(q)
        level3(q)
        sums(q - 1, 2)
        sums(q - 2, 4)
        if q + 2 < PHASES:
            level0(q + 2)
        if q + 1 < PHASES:
            level1(q + 1)
        level4(q)
        sums(q - 1, 3)
        sums(q - 2, 5)
        mate_arrived(q)
        multiply(q)
        sums(q, 1)
    sums(PHASES - 2, 4)
    sums(PHASES - 1, 2)
    sums(PHASES - 2, 5)
    sums(PHASES - 1, 3)
    sums(PHASES - 1, 4)
    for q in range(PHASES):
        drain(q)
    sums(PHASES - 1, 5)


def solution(mesh):
    devices, planes = mesh.shape["row"], mesh.shape["col"]

    def body(vectors, basis, block_units):
        rows, depth = vectors.shape
        own = basis.shape[1]
        step = own // PHASES
        width = step * devices
        chunk = width // planes
        f32, bf16 = jnp.float32, jnp.bfloat16
        summed = pl.pallas_call(
            functools.partial(kernel, (rows, depth, own, devices, planes)),
            out_shape=jax.ShapeDtypeStruct((own * devices // planes, rows), f32),
            in_specs=[
                pl.BlockSpec(memory_space=pltpu.SMEM),
                pl.BlockSpec(memory_space=pl.ANY),
                pl.BlockSpec(memory_space=pl.ANY),
            ],
            out_specs=pl.BlockSpec(memory_space=pltpu.VMEM),
            scratch_shapes=[
                pltpu.VMEM((PHASES, width, depth), f32),
                pltpu.VMEM((rows, depth), f32),
                pltpu.VMEM((3 * depth, rows), bf16),
                pltpu.VMEM((width, 3 * depth), bf16),
                pltpu.VMEM((PHASES, width, rows), f32),
                pltpu.VMEM((PHASES, chunk // 2, rows), f32),
                pltpu.VMEM((PHASES, 3, chunk, rows), f32),
                pltpu.VMEM((PHASES, chunk // 2, rows), f32),
                pltpu.VMEM((PHASES, 3, chunk, rows), f32),
                pltpu.SemaphoreType.DMA,
                pltpu.SemaphoreType.DMA((PHASES,)),
                pltpu.SemaphoreType.DMA((PHASES, 2, RINGS * RINGS)),
                pltpu.SemaphoreType.DMA((PHASES,)),
                pltpu.SemaphoreType.DMA((PHASES,)),
                pltpu.SemaphoreType.DMA((PHASES,)),
                pltpu.SemaphoreType.DMA((PHASES, 2, 4)),
                pltpu.SemaphoreType.DMA((PHASES, 2, 4)),
            ],
            compiler_params=pltpu.CompilerParams(
                collective_id=0, has_side_effects=True, vmem_limit_bytes=63 * 1024 * 1024
            ),
            cost_estimate=pl.CostEstimate(
                flops=6 * rows * depth * own * devices, bytes_accessed=4 * rows * depth, transcendentals=0
            ),
        )(block_units, vectors, basis.T)
        return summed.T

    return jax.shard_map(
        body,
        mesh=mesh,
        in_specs=(P("row", "col"), P("col", "row"), P()),
        out_specs=P("row", "col"),
        check_vma=False,
    )
```

time: 191 us -> 128 us (0.67); the launches traced: 188 us -> 128 us
  waiting for transfers between devices: 134 us -> 0 us
  Pallas kernels: 0 us -> 125 us
  matrix products: 31.9 us -> 0 us
  between operations: 14.7 us -> 0.01 us
  other arithmetic: 2.96 us -> 0 us
  local copies, waits for them, and re-layouts: 4.57 us -> 2.04 us
    pallas_call x0 -> x1, Pallas kernels: none -> 125 us  [body(): pl.pallas_call(functools.partial(kernel, (rows, depth, own, devices, plan...]
    select_n x1 -> x0, waiting for transfers between devices: 80.3 us -> none  [reference(): jnp.where(row_block[:, None] == slab_block[None, :], basis, jnp.float32(0...]
    unnamed x3 -> x0, waiting for transfers between devices: 53.3 us -> none
    dot_general x1 -> x0, matrix products: 31.9 us -> none  [reference(): jnp.dot(vectors, masked, precision=lax.Precision.HIGHEST, preferred_eleme...]
    transpose x0 -> x1, local copies, waits for them, and re-layouts: none -> 2.04 us  [body(): return summed.T]
    dot_general x1 -> x0, local copies, waits for them, and re-layouts: 2.04 us -> none  [reference(): jnp.dot(vectors, masked, precision=lax.Precision.HIGHEST, preferred_eleme...]
    select_n x1 -> x0, other arithmetic: 1.94 us -> none  [reference(): jnp.where(row_block[:, None] == slab_block[None, :], basis, jnp.float32(0...]
  transfers between devices with their start and end apart: 2 -> 0, of which waited for: 2 -> 0; matrix products, arithmetic and copies ran while one was open for 0% -> 0% of each run, Pallas kernels for 0% -> 0%
where the time goes in v1:
time: 128 us
  Pallas kernels  125 us (98%)
  local copies, waits for them, and re-layouts  2.04 us (2%)
    pallas_call x1, Pallas kernels, body(): pl.pallas_call(functools.partial(kernel, (rows, depth, own, devices, plan...  125 us

profile of v1, /device:TPU:32, one launch (start us, length us, event | category | flops | bytes accessed | tf_op | source)
XLA Modules:
  0.0 127.5 jit_solution(14214401135514737524)
XLA Ops:
  0.0 125.5 %shard_map.37 = f32[256,512]{1,0:T(8,128)} custom-call(s32[8]{0:T(128)} %units_ref.1, f32[512,2048]{1,0:T(8,128)} %v_hbm.1, f32[64,2048]{1,0:T(8,128)} %bitcast.3), custom_call_target="tpu_custom_call" | custom-call | flops 12884901888 | bytes 4194304 | tf_op jit(solution)/shard_map/pallas_call | solution.py:309
  125.5 2.0 %copy.4 = f32[512,256]{1,0:T(8,128)} copy(f32[512,256]{0,1:T(8,128)} %bitcast.2) | data formatting | bytes 1048576 | tf_op jit(solution)/shard_map/transpose | solution.py:344

commit v2 on v1

--- a/solution.py
+++ b/solution.py
@@ -12,6 +12,9 @@
 START = 7168
 RINGS = 4
 PHASES = 8
+AHEAD = 2
+LAG = 0
+HOP_ORDER = (1, 2, 3, 4)
 
 
 def kernel(dims, units_ref, v_hbm, bt_hbm, o_ref, gathered, v_mem, weights, lhs, part, up_first, up_rest, down_first,
@@ -111,43 +114,23 @@
         for h in range(2):
             share(q, h, 0, 0)
 
-    def along_second(q, h, fo):
-        for direction in (1, -1):
-            send(q, h, fo, 0, 1, direction)
-        share(q, h, fo, 0)
-
-    def level1(q):
-        for fo in (-1, 1):
+    hops = [[] for _ in range(5)]
+    for fo in (0, -1, 1, 2):
+        for so in (0, -1, 1, 2):
+            hops[abs(fo) + abs(so)].append((fo, so))
+
+    def pass_on(q, hop):
+        for fo, so in hops[hop]:
             for h in range(2):
-                arrived(q, h, fo, 0)
-                if first_way(q, h) == -fo:
-                    send(q, h, fo, 0, 0, -fo)
-                along_second(q, h, fo)
-
-    def cross(q, h, fo):
-        for so in (-1, 1):
-            arrived(q, h, fo, so)
-            if second_way(q, h, fo) == -so:
-                send(q, h, fo, so, 1, -so)
-            share(q, h, fo, so)
-
-    def level2(q):
-        for h in range(2):
-            cross(q, h, 0)
-        for h in range(2):
-            arrived(q, h, 2, 0)
-            along_second(q, h, 2)
-
-    def level3(q):
-        for fo in (-1, 1, 2):
-            for h in range(2):
-                cross(q, h, fo)
-
-    def level4(q):
-        for fo in (0, -1, 1, 2):
-            for h in range(2):
-                arrived(q, h, fo, 2)
-                share(q, h, fo, 2)
+                arrived(q, h, fo, so)
+                if so == 0:
+                    if abs(fo) == 1 and first_way(q, h) == -fo:
+                        send(q, h, fo, so, 0, -fo)
+                    for direction in (1, -1):
+                        send(q, h, fo, so, 1, direction)
+                elif abs(so) == 1 and second_way(q, h, fo) == -so:
+                    send(q, h, fo, so, 1, -so)
+                share(q, h, fo, so)
 
     def prepare():
         load_v.wait()
@@ -267,30 +250,26 @@
         ref = gathered.at[q, pl.ds(0, RINGS * RINGS * step)]
         pltpu.make_async_copy(ref, ref, mate_sem.at[q]).wait()
 
-    level0(0)
-    level0(1)
+    for q in range(AHEAD):
+        level0(q)
     prepare()
-    level1(0)
-    for q in range(PHASES):
-        level2(q)
-        level3(q)
-        sums(q - 1, 2)
-        sums(q - 2, 4)
-        if q + 2 < PHASES:
-            level0(q + 2)
-        if q + 1 < PHASES:
-            level1(q + 1)
-        level4(q)
-        sums(q - 1, 3)
-        sums(q - 2, 5)
-        mate_arrived(q)
-        multiply(q)
-        sums(q, 1)
-    sums(PHASES - 2, 4)
-    sums(PHASES - 1, 2)
-    sums(PHASES - 2, 5)
-    sums(PHASES - 1, 3)
-    sums(PHASES - 1, 4)
+    for tick in range(PHASES + 3 + LAG):
+        for hop in HOP_ORDER:
+            q = tick - (hop - 1)
+            if 0 <= q < PHASES:
+                pass_on(q, hop)
+        if tick + AHEAD < PHASES:
+            level0(tick + AHEAD)
+        done = tick - 3
+        for s in (5, 4, 3, 2):
+            sums(done - s + 1 - LAG, s)
+        if 0 <= done - LAG < PHASES:
+            mate_arrived(done - LAG)
+            multiply(done - LAG)
+            sums(done - LAG, 1)
+    for extra in range(1, 4):
+        for s in (5, 4, 3, 2):
+            sums(PHASES - 1 + extra - s + 1, s)
     for q in range(PHASES):
         drain(q)
     sums(PHASES - 1, 5)

time: 128 us -> 95.3 us (0.74)
  Pallas kernels: 125 us -> 93.1 us
    pallas_call x1, Pallas kernels: 125 us -> 93.1 us  [body(): pl.pallas_call(functools.partial(kernel, (rows, depth, own, devices, plan...]
where the time goes in v2:
time: 95.3 us; the launch traced here: 95.2 us
  Pallas kernels  93.1 us (98%)
  local copies, waits for them, and re-layouts  2.04 us (2%)
    pallas_call x1, Pallas kernels, body(): pl.pallas_call(functools.partial(kernel, (rows, depth, own, devices, plan...  93.1 us
    transpose x1, local copies, waits for them, and re-layouts, body(): return summed.T  2.04 us

profile of v2, /device:TPU:32, one launch (start us, length us, event | category | flops | bytes accessed | tf_op | source)
XLA Modules:
  0.0 95.2 jit_solution(5113471219765386158)
XLA Ops:
  0.0 93.1 %shard_map.37 = f32[256,512]{1,0:T(8,128)} custom-call(s32[8]{0:T(128)} %units_ref.1, f32[512,2048]{1,0:T(8,128)} %v_hbm.1, f32[64,2048]{1,0:T(8,128)} %bitcast.3), custom_call_target="tpu_custom_call" | custom-call | flops 12884901888 | bytes 4194304 | tf_op jit(solution)/shard_map/pallas_call | solution.py:288
  93.1 2.0 %copy.4 = f32[512,256]{1,0:T(8,128)} copy(f32[512,256]{0,1:T(8,128)} %bitcast.2) | data formatting | bytes 1048576 | tf_op jit(solution)/shard_map/transpose | solution.py:323

commit v3 on v0

v3 whole, which is shorter than its diff:
```python
import functools

import jax
import jax.numpy as jnp
from jax import lax
from jax.experimental import pallas as pl
from jax.experimental.pallas import tpu as pltpu
from jax.sharding import PartitionSpec as P

MESH = pl.DeviceIdType.MESH
UNIT = 256
START = 7168
RINGS = 4
SIZES = (16, 16, 16, 16)
ORDER = (
    (0, 0, 0, 0, 0), (2, 0, 0, 0, 0), (0, 1, 0, 0, 0), (1, 0, 1, -1, 0), (1, 0, 1, 1, 0), (1, 0, 0, -1, 0), (1, 0, 0, 1, 0),
    (1, 0, 0, 0, -1), (1, 0, 0, 0, 1), (1, 0, 1, 0, -1), (1, 0, 1, 0, 1), (1, 1, 1, -1, 0), (1, 1, 1, 1, 0),
    (1, 1, 0, -1, 0), (1, 1, 0, 1, 0), (1, 1, 0, 0, -1), (1, 1, 0, 0, 1), (1, 1, 1, 0, -1), (1, 1, 1, 0, 1),
    (1, 0, 0, -1, -1), (1, 0, 1, 2, 0), (1, 0, 1, -1, -1), (1, 0, 1, -1, 1), (1, 0, 0, 1, -1), (1, 0, 0, -1, 1),
    (1, 0, 1, 1, -1), (1, 0, 1, 1, 1), (1, 0, 0, 0, 2), (1, 0, 0, 1, 1), (1, 0, 0, 2, 0), (1, 1, 1, -1, 1), (3, 0, 0, 0, 0),
    (1, 0, 1, 0, 2), (1, 1, 1, 2, 0), (1, 1, 0, -1, 1), (1, 1, 1, 1, 1), (1, 1, 0, -1, -1), (1, 1, 0, 1, 1),
    (1, 1, 1, -1, -1), (1, 1, 0, 2, 0), (1, 1, 0, 1, -1), (1, 1, 0, 0, 2), (1, 1, 1, 1, -1), (1, 1, 1, 0, 2),
    (4, 0, 0, 2, 0), (1, 0, 0, -1, 2), (1, 0, 0, 1, 2), (1, 0, 1, 2, -1), (1, 0, 1, 2, 1), (3, 1, 0, 0, 0), (0, 2, 0, 0, 0),
    (1, 0, 0, 2, -1), (1, 0, 0, 2, 1), (1, 0, 1, -1, 2), (1, 0, 1, 1, 2), (3, 0, -1, 0, 0), (1, 1, 0, 2, -1),
    (1, 1, 0, -1, 2), (1, 1, 1, 2, -1), (1, 1, 1, -1, 2), (3, 0, 1, 0, 0), (4, 0, 0, 3, 0), (1, 1, 0, 1, 2),
    (1, 1, 0, 2, 1), (1, 1, 1, 2, 1), (1, 1, 1, 1, 2), (3, 1, -1, 0, 0), (0, 3, 0, 0, 0), (4, 1, 0, 2, 0), (1, 0, 1, 2, 2),
    (1, 2, 1, -1, 0), (1, 2, 1, 1, 0), (4, 0, -1, 2, 0), (1, 2, 0, -1, 0), (3, 1, 1, 0, 0), (4, 0, 1, 2, 0),
    (1, 2, 0, 0, -1), (1, 2, 0, 0, 1), (1, 2, 1, 0, -1), (1, 2, 0, 1, 0), (4, 0, 0, 4, 0), (1, 1, 0, 2, 2), (1, 0, 0, 2, 2),
    (1, 1, 1, 2, 2), (1, 2, 1, 0, 1), (4, 1, -1, 2, 0), (4, 1, 0, 3, 0), (1, 3, 1, -1, 0), (1, 3, 1, 1, 0),
    (1, 3, 0, -1, 0), (1, 3, 0, 1, 0), (3, 0, 2, 0, 0), (4, 0, -1, 3, 0), (4, 1, 1, 2, 0), (4, 0, 1, 3, 0),
    (1, 3, 0, 0, -1), (1, 3, 0, 0, 1), (1, 3, 1, 0, -1), (1, 3, 1, 0, 1), (3, 1, 2, 0, 0), (4, 0, 0, 5, 0),
    (4, 1, -1, 3, 0), (1, 2, 1, 2, 0), (1, 2, 0, -1, -1), (1, 2, 1, -1, -1), (1, 2, 1, -1, 1), (4, 1, 0, 4, 0),
    (1, 2, 0, 0, 2), (1, 2, 0, -1, 1), (1, 2, 1, 1, -1), (1, 2, 1, 1, 1), (4, 0, 2, 2, 0), (3, 2, 0, 0, 0),
    (4, 0, -1, 4, 0), (4, 1, 1, 3, 0), (1, 2, 0, 1, -1), (4, 0, 1, 4, 0), (4, 1, 2, 2, 0), (1, 2, 0, 1, 1), (1, 2, 0, 2, 0),
    (1, 2, 1, 0, 2), (1, 3, 1, 2, 0), (1, 3, 1, -1, 1), (1, 3, 0, -1, 1), (1, 3, 1, 1, 1), (4, 1, -1, 4, 0),
    (1, 3, 0, -1, -1), (1, 3, 0, 1, 1), (1, 3, 1, -1, -1), (1, 3, 0, 2, 0), (4, 1, 0, 5, 0), (4, 0, 2, 3, 0),
    (4, 2, 0, 2, 0), (1, 3, 0, 0, 2), (1, 3, 0, 1, -1), (1, 3, 1, 1, -1), (1, 3, 1, 0, 2), (4, 0, -1, 5, 0),
    (1, 2, 0, -1, 2), (1, 2, 0, 1, 2), (1, 2, 1, 2, -1), (1, 2, 1, 2, 1), (3, 3, 0, 0, 0), (4, 1, 1, 4, 0), (4, 0, 1, 5, 0),
    (1, 2, 0, 2, -1), (1, 2, 0, 2, 1), (1, 2, 1, -1, 2), (1, 2, 1, 1, 2), (3, 2, -1, 0, 0), (4, 1, 2, 3, 0),
    (4, 1, -1, 5, 0), (1, 3, 0, -1, 2), (1, 3, 1, 2, -1), (4, 0, 2, 4, 0), (1, 3, 1, 2, 1), (1, 3, 0, 2, -1),
    (3, 2, 1, 0, 0), (4, 2, 0, 3, 0), (4, 3, 0, 2, 0), (1, 3, 0, 1, 2), (1, 3, 0, 2, 1), (1, 3, 1, 1, 2), (1, 3, 1, -1, 2),
    (3, 3, -1, 0, 0), (4, 1, 1, 5, 0), (4, 2, -1, 2, 0), (1, 2, 0, 2, 2), (1, 2, 1, 2, 2), (3, 3, 1, 0, 0), (4, 1, 2, 4, 0),
    (1, 3, 1, 2, 2), (4, 2, 1, 2, 0), (4, 0, 2, 5, 0), (1, 3, 0, 2, 2), (3, 2, 2, 0, 0), (4, 2, 0, 4, 0), (3, 3, 2, 0, 0),
    (4, 3, -1, 2, 0), (4, 3, 0, 3, 0), (4, 2, -1, 3, 0), (4, 3, 1, 2, 0), (4, 1, 2, 5, 0), (4, 2, 2, 2, 0), (4, 2, 1, 3, 0),
    (4, 2, 0, 5, 0), (4, 3, 2, 2, 0), (4, 3, -1, 3, 0), (4, 3, 0, 4, 0), (4, 2, -1, 4, 0), (4, 3, 1, 3, 0), (4, 2, 2, 3, 0),
    (4, 2, 1, 4, 0), (4, 3, 2, 3, 0), (4, 3, -1, 4, 0), (4, 3, 0, 5, 0), (4, 2, -1, 5, 0), (4, 3, 1, 4, 0), (4, 2, 2, 4, 0),
    (4, 2, 1, 5, 0), (4, 3, 2, 4, 0), (4, 3, -1, 5, 0), (4, 3, 1, 5, 0), (4, 2, 2, 5, 0), (4, 3, 2, 5, 0),
)


def kernel(dims, units_ref, v_hbm, bt_hbm, o_ref, gathered, v_mem, weights, lhs, part, brought, local_sem, own_sem,
           gather_sem, gather_sent, mate_sem, mate_sent, sum_sem, sum_sent):
    rows, depth, own, planes = dims
    half = depth // 2
    offsets = [sum(SIZES[:q]) for q in range(len(SIZES))]

    me = lax.axis_index("row")
    z = lax.axis_index("col")
    core = lax.rem(me, 2)
    x = lax.rem(lax.div(me, 2), RINGS)
    y = lax.div(me, 2 * RINGS)

    def shift(c, by, n):
        return lax.rem(c + (by % n), n)

    def device(xx, yy):
        return (yy * RINGS + xx) * 2 + core

    mate_id = (me + 1 - 2 * core, z)
    neighbour = {
        ("x", 1): (device(shift(x, 1, RINGS), y), z),
        ("x", -1): (device(shift(x, -1, RINGS), y), z),
        ("y", 1): (device(x, shift(y, 1, RINGS)), z),
        ("y", -1): (device(x, shift(y, -1, RINGS)), z),
    }
    along_z = {1: (me, shift(z, 1, planes)), -1: (me, shift(z, -1, planes))}
    axes = (("x", "y"), ("y", "x"))

    def slot(q, xx, yy):
        step = SIZES[q]
        return pl.multiple_of(offsets[q] * 2 * RINGS * RINGS + ((xx * RINGS + yy) * 2 + core) * step, 8)

    def own_copy(q):
        step = SIZES[q]
        return pltpu.make_async_copy(
            bt_hbm.at[pl.ds(offsets[q], step)], gathered.at[pl.ds(slot(q, x, y), step)], own_sem.at[q]
        )

    for q in range(len(SIZES)):
        own_copy(q).start()
    load_v = pltpu.make_async_copy(v_hbm, v_mem, local_sem)
    load_v.start()

    barrier = pltpu.get_barrier_semaphore()
    for other in (*neighbour.values(), mate_id, *along_z.values()):
        pl.semaphore_signal(barrier, inc=1, device_id=other, device_id_type=MESH)
    pl.semaphore_wait(barrier, 7)

    def piece(q, h, fo, so):
        dx, dy = (fo, so) if h == 0 else (so, fo)
        first = slot(q, shift(x, dx, RINGS), shift(y, dy, RINGS))
        return gathered.at[pl.ds(first, SIZES[q]), pl.ds(h * half, half)]

    def send(q, h, fo, so, which, direction):
        ref = piece(q, h, fo, so)
        nfo, nso = (fo - direction, so) if which == 0 else (fo, so - direction)
        pltpu.make_async_remote_copy(
            src_ref=ref,
            dst_ref=ref,
            send_sem=gather_sent,
            recv_sem=gather_sem.at[q, h, (nfo % RINGS) * RINGS + nso % RINGS],
            device_id=neighbour[axes[h][which], direction],
            device_id_type=MESH,
        ).start()

    def share(q, h, fo, so):
        ref = piece(q, h, fo, so)
        dx = (fo if h == 0 else so) % RINGS
        pltpu.make_async_remote_copy(
            src_ref=ref,
            dst_ref=ref,
            send_sem=mate_sent,
            recv_sem=mate_sem.at[q, dx],
            device_id=mate_id,
            device_id_type=MESH,
        ).start()

    def begin(q):
        own_copy(q).wait()
        for h in (1, 0):
            for direction in (1, -1):
                send(q, h, 0, 0, 1 - h, direction)
        for h in (0, 1):
            for direction in (1, -1):
                send(q, h, 0, 0, h, direction)
        for h in range(2):
            share(q, h, 0, 0)

    def pass_on(q, h, fo, so):
        ref = piece(q, h, fo, so)
        pltpu.make_async_copy(ref, ref, gather_sem.at[q, h, (fo % RINGS) * RINGS + so % RINGS]).wait()
        if so == 0:
            if abs(fo) == 1 and (1 if (q + h) % 2 == 0 else -1) == -fo:
                send(q, h, fo, so, 0, -fo)
            for direction in (1, -1):
                send(q, h, fo, so, 1, direction)
        elif abs(so) == 1 and (1 if (q + fo // 2 + fo) % 2 == 0 else -1) == -so:
            send(q, h, fo, so, 1, -so)
        share(q, h, fo, so)

    def prepare():
        load_v.wait()
        tile = 256

        def body(t, _):
            at_k = pl.multiple_of(t * tile, tile)
            block = v_mem[:, pl.ds(at_k, tile)].T
            hi = block.astype(jnp.bfloat16)
            lo = (block - hi.astype(jnp.float32)).astype(jnp.bfloat16)
            weights[pl.ds(at_k, tile), :] = hi
            weights[pl.ds(pl.multiple_of(depth + at_k, tile), tile), :] = lo
            weights[pl.ds(pl.multiple_of(2 * depth + at_k, tile), tile), :] = hi
            return 0

        lax.fori_loop(0, depth // tile, body, 0)

    ends = []
    total = 0
    for b in range(7):
        total = total + units_ref[b] * UNIT
        ends.append(total)

    def block_of(position):
        ids = jnp.zeros_like(position)
        for end in ends:
            ids = ids + (position >= end).astype(jnp.int32)
        return ids

    def group_first(q, dx):
        step = SIZES[q]
        return pl.multiple_of(
            offsets[q] * 2 * RINGS * RINGS + shift(x, dx, RINGS) * (2 * RINGS * step), 2 * RINGS * 8
        )

    def multiply(q, dx):
        step = SIZES[q]
        width = 2 * RINGS * step
        first = group_first(q, dx)
        ref = gathered.at[pl.ds(0, RINGS * step)]
        pltpu.make_async_copy(ref, ref, mate_sem.at[q, dx % RINGS]).wait()
        xx = shift(x, dx, RINGS)
        row_block = block_of(z * depth + lax.broadcasted_iota(jnp.int32, (1, depth), 1))
        batch = 16

        def split(g, _):
            at_row = pl.multiple_of(g * batch, batch)
            index = at_row + lax.broadcasted_iota(jnp.int32, (batch, 1), 0)
            chip = lax.div(index, 2 * step) * RINGS + xx
            owner = chip * 2 + lax.rem(lax.div(index, step), 2)
            column = owner * own + offsets[q] + lax.rem(index, step)
            keep = block_of(START + column) == row_block
            block = jnp.where(keep, gathered[pl.ds(pl.multiple_of(first + at_row, batch), batch), :], 0.0)
            hi = block.astype(jnp.bfloat16)
            lo = (block - hi.astype(jnp.float32)).astype(jnp.bfloat16)
            lhs[pl.ds(at_row, batch), 0:depth] = hi
            lhs[pl.ds(at_row, batch), depth:2 * depth] = hi
            lhs[pl.ds(at_row, batch), 2 * depth:3 * depth] = lo
            return 0

        lax.fori_loop(0, width // batch, split, 0)
        across = 256

        def product(m, _):
            lanes = pl.ds(pl.multiple_of(m * across, across), across)
            part[pl.ds(first, width), lanes] = jnp.dot(
                lhs[0:width, :], weights[:, lanes], preferred_element_type=jnp.float32
            )
            return 0

        lax.fori_loop(0, rows // across, product, 0)

    def add_up(q, dx, s):
        step = SIZES[q]
        chunk = 2 * step
        xx = shift(x, dx, RINGS)
        side = lax.div(xx, 2)
        odd = lax.rem(z + side, 2)
        near = lax.rem(lax.div(z - side + 9, 2), RINGS)
        first = group_first(q, dx)
        slot_first = offsets[q] * 2 * RINGS + (dx % RINGS) * chunk

        def rows_of(j, start, size):
            return pl.ds(pl.multiple_of(first + shift(near, j, RINGS) * chunk + start, 8), size)

        def wait_for(lane, slot_at, size):
            ref = brought.at[lane, slot_at, pl.ds(slot_first, size)]
            pltpu.make_async_copy(ref, ref, sum_sem.at[q, dx % RINGS, lane * 2 + slot_at]).wait()

        def send_on(lane, slot_at, src, size):
            pltpu.make_async_remote_copy(
                src_ref=part.at[src],
                dst_ref=brought.at[lane, slot_at, pl.ds(slot_first, size)],
                send_sem=sum_sent,
                recv_sem=sum_sem.at[q, dx % RINGS, lane * 2 + slot_at],
                device_id=along_z[1 - 2 * lane],
                device_id_type=MESH,
            ).start()

        @pl.when(odd == (s + 1) % 2)
        def _():
            if s == 5:
                for lane in range(2):
                    wait_for(lane, 1, chunk)
                where = pl.ds(slot_first, chunk)
                final = part[rows_of(0, 0, chunk), :] + brought[0, 1, where, :] + brought[1, 1, where, :]
                for i in range(2):
                    to = pl.multiple_of(lax.rem(xx, 2) * (2 * own) + i * own + offsets[q], 8)
                    o_ref[pl.ds(to, step), :] = final[i * step:(i + 1) * step, :]
                return
            for lane in range(2):
                start = lane * step
                j = {1: (2, 2), 2: (1, -2), 3: (1, -1), 4: (0, -1)}[s][lane]
                if s == 1:
                    send_on(lane, 0, rows_of(j, start, step), step)
                    continue
                if s == 2:
                    wait_for(lane, 0, step)
                    where = rows_of(j, start, step)
                    part[where, :] = part[where, :] + brought[lane, 0, pl.ds(slot_first, step), :]
                else:
                    wait_for(lane, s - 3, chunk)
                    where = rows_of(j, 0, chunk)
                    part[where, :] = part[where, :] + brought[lane, s - 3, pl.ds(slot_first, chunk), :]
                send_on(lane, 0 if s == 2 else 1, rows_of(j, 0, chunk), chunk)

    for op, q, a, b, c in ORDER:
        if op == 0:
            begin(q)
        elif op == 1:
            pass_on(q, a, b, c)
        elif op == 2:
            prepare()
        elif op == 3:
            multiply(q, a)
            add_up(q, a, 1)
        else:
            add_up(q, a, b)

    ref = gathered.at[pl.ds(0, (RINGS * RINGS - 1) * own)]
    pltpu.make_async_copy(ref, ref, gather_sent).wait()
    ref = gathered.at[pl.ds(0, RINGS * RINGS * own)]
    pltpu.make_async_copy(ref, ref, mate_sent).wait()
    ref = part.at[pl.ds(0, 28 * own)]
    pltpu.make_async_copy(ref, ref, sum_sent).wait()


def solution(mesh):
    devices, planes = mesh.shape["row"], mesh.shape["col"]
    phases = len(SIZES)

    def body(vectors, basis, block_units):
        rows, depth = vectors.shape
        own = basis.shape[1]
        f32, bf16 = jnp.float32, jnp.bfloat16
        dma = pltpu.SemaphoreType.DMA
        summed = pl.pallas_call(
            functools.partial(kernel, (rows, depth, own, planes)),
            out_shape=jax.ShapeDtypeStruct((own * devices // planes, rows), f32),
            in_specs=[
                pl.BlockSpec(memory_space=pltpu.SMEM),
                pl.BlockSpec(memory_space=pl.ANY),
                pl.BlockSpec(memory_space=pl.ANY),
            ],
            out_specs=pl.BlockSpec(memory_space=pltpu.VMEM),
            scratch_shapes=[
                pltpu.VMEM((own * devices, depth), f32),
                pltpu.VMEM((rows, depth), f32),
                pltpu.VMEM((3 * depth, rows), bf16),
                pltpu.VMEM((2 * RINGS * max(SIZES), 3 * depth), bf16),
                pltpu.VMEM((own * devices, rows), f32),
                pltpu.VMEM((2, 2, 2 * RINGS * own, rows), f32),
                dma,
                dma((phases,)),
                dma((phases, 2, RINGS * RINGS)),
                dma,
                dma((phases, RINGS)),
                dma,
                dma((phases, RINGS, 4)),
                dma,
            ],
            compiler_params=pltpu.CompilerParams(
                collective_id=0, has_side_effects=True, vmem_limit_bytes=63 * 1024 * 1024
            ),
            cost_estimate=pl.CostEstimate(
                flops=6 * rows * depth * own * devices, bytes_accessed=4 * rows * depth, transcendentals=0
            ),
        )(block_units, vectors, basis.T)
        return summed.T

    return jax.shard_map(
        body,
        mesh=mesh,
        in_specs=(P("row", "col"), P("col", "row"), P()),
        out_specs=P("row", "col"),
        check_vma=False,
    )
```

time: 191 us -> 84.9 us (0.44); the launches traced: 188 us -> 84.8 us
  waiting for transfers between devices: 134 us -> 0 us
  Pallas kernels: 0 us -> 82.7 us
  matrix products: 31.9 us -> 0 us
  between operations: 14.7 us -> 0.01 us
  other arithmetic: 2.96 us -> 0 us
  local copies, waits for them, and re-layouts: 4.57 us -> 2.04 us
    pallas_call x0 -> x1, Pallas kernels: none -> 82.7 us  [body(): pl.pallas_call(functools.partial(kernel, (rows, depth, own, planes)), out...]
    select_n x1 -> x0, waiting for transfers between devices: 80.3 us -> none  [reference(): jnp.where(row_block[:, None] == slab_block[None, :], basis, jnp.float32(0...]
    unnamed x3 -> x0, waiting for transfers between devices: 53.3 us -> none
    dot_general x1 -> x0, matrix products: 31.9 us -> none  [reference(): jnp.dot(vectors, masked, precision=lax.Precision.HIGHEST, preferred_eleme...]
    transpose x0 -> x1, local copies, waits for them, and re-layouts: none -> 2.04 us  [body(): return summed.T]
    dot_general x1 -> x0, local copies, waits for them, and re-layouts: 2.04 us -> none  [reference(): jnp.dot(vectors, masked, precision=lax.Precision.HIGHEST, preferred_eleme...]
    select_n x1 -> x0, other arithmetic: 1.94 us -> none  [reference(): jnp.where(row_block[:, None] == slab_block[None, :], basis, jnp.float32(0...]
  transfers between devices with their start and end apart: 2 -> 0, of which waited for: 2 -> 0; matrix products, arithmetic and copies ran while one was open for 0% -> 0% of each run, Pallas kernels for 0% -> 0%
where the time goes in v3:
time: 84.9 us; the launch traced here: 84.8 us
  Pallas kernels  82.7 us (97%)
  local copies, waits for them, and re-layouts  2.04 us (2%)
    pallas_call x1, Pallas kernels, body(): pl.pallas_call(functools.partial(kernel, (rows, depth, own, planes)), out...  82.7 us
    transpose x1, local copies, waits for them, and re-layouts, body(): return summed.T  2.04 us

profile of v3, /device:TPU:32, one launch (start us, length us, event | category | flops | bytes accessed | tf_op | source)
XLA Modules:
  0.0 84.8 jit_solution(13838446256995044682)
XLA Ops:
  0.0 82.7 %shard_map.37 = f32[256,512]{1,0:T(8,128)} custom-call(s32[8]{0:T(128)} %units_ref.1, f32[512,2048]{1,0:T(8,128)} %v_hbm.1, f32[64,2048]{1,0:T(8,128)} %bitcast.3), custom_call_target="tpu_custom_call" | custom-call | flops 12884901888 | bytes 4194304 | tf_op jit(solution)/shard_map/pallas_call | solution.py:306
  82.7 2.0 %copy.4 = f32[512,256]{1,0:T(8,128)} copy(f32[512,256]{0,1:T(8,128)} %bitcast.2) | data formatting | bytes 1048576 | tf_op jit(solution)/shard_map/transpose | solution.py:338

commit v4 on v3

--- a/solution.py
+++ b/solution.py
@@ -20,31 +20,31 @@
     (1, 0, 1, 1, -1), (1, 0, 1, 1, 1), (1, 0, 0, 0, 2), (1, 0, 0, 1, 1), (1, 0, 0, 2, 0), (1, 1, 1, -1, 1), (3, 0, 0, 0, 0),
     (1, 0, 1, 0, 2), (1, 1, 1, 2, 0), (1, 1, 0, -1, 1), (1, 1, 1, 1, 1), (1, 1, 0, -1, -1), (1, 1, 0, 1, 1),
     (1, 1, 1, -1, -1), (1, 1, 0, 2, 0), (1, 1, 0, 1, -1), (1, 1, 0, 0, 2), (1, 1, 1, 1, -1), (1, 1, 1, 0, 2),
-    (4, 0, 0, 2, 0), (1, 0, 0, -1, 2), (1, 0, 0, 1, 2), (1, 0, 1, 2, -1), (1, 0, 1, 2, 1), (3, 1, 0, 0, 0), (0, 2, 0, 0, 0),
-    (1, 0, 0, 2, -1), (1, 0, 0, 2, 1), (1, 0, 1, -1, 2), (1, 0, 1, 1, 2), (3, 0, -1, 0, 0), (1, 1, 0, 2, -1),
-    (1, 1, 0, -1, 2), (1, 1, 1, 2, -1), (1, 1, 1, -1, 2), (3, 0, 1, 0, 0), (4, 0, 0, 3, 0), (1, 1, 0, 1, 2),
-    (1, 1, 0, 2, 1), (1, 1, 1, 2, 1), (1, 1, 1, 1, 2), (3, 1, -1, 0, 0), (0, 3, 0, 0, 0), (4, 1, 0, 2, 0), (1, 0, 1, 2, 2),
-    (1, 2, 1, -1, 0), (1, 2, 1, 1, 0), (4, 0, -1, 2, 0), (1, 2, 0, -1, 0), (3, 1, 1, 0, 0), (4, 0, 1, 2, 0),
-    (1, 2, 0, 0, -1), (1, 2, 0, 0, 1), (1, 2, 1, 0, -1), (1, 2, 0, 1, 0), (4, 0, 0, 4, 0), (1, 1, 0, 2, 2), (1, 0, 0, 2, 2),
-    (1, 1, 1, 2, 2), (1, 2, 1, 0, 1), (4, 1, -1, 2, 0), (4, 1, 0, 3, 0), (1, 3, 1, -1, 0), (1, 3, 1, 1, 0),
-    (1, 3, 0, -1, 0), (1, 3, 0, 1, 0), (3, 0, 2, 0, 0), (4, 0, -1, 3, 0), (4, 1, 1, 2, 0), (4, 0, 1, 3, 0),
-    (1, 3, 0, 0, -1), (1, 3, 0, 0, 1), (1, 3, 1, 0, -1), (1, 3, 1, 0, 1), (3, 1, 2, 0, 0), (4, 0, 0, 5, 0),
-    (4, 1, -1, 3, 0), (1, 2, 1, 2, 0), (1, 2, 0, -1, -1), (1, 2, 1, -1, -1), (1, 2, 1, -1, 1), (4, 1, 0, 4, 0),
-    (1, 2, 0, 0, 2), (1, 2, 0, -1, 1), (1, 2, 1, 1, -1), (1, 2, 1, 1, 1), (4, 0, 2, 2, 0), (3, 2, 0, 0, 0),
-    (4, 0, -1, 4, 0), (4, 1, 1, 3, 0), (1, 2, 0, 1, -1), (4, 0, 1, 4, 0), (4, 1, 2, 2, 0), (1, 2, 0, 1, 1), (1, 2, 0, 2, 0),
-    (1, 2, 1, 0, 2), (1, 3, 1, 2, 0), (1, 3, 1, -1, 1), (1, 3, 0, -1, 1), (1, 3, 1, 1, 1), (4, 1, -1, 4, 0),
-    (1, 3, 0, -1, -1), (1, 3, 0, 1, 1), (1, 3, 1, -1, -1), (1, 3, 0, 2, 0), (4, 1, 0, 5, 0), (4, 0, 2, 3, 0),
-    (4, 2, 0, 2, 0), (1, 3, 0, 0, 2), (1, 3, 0, 1, -1), (1, 3, 1, 1, -1), (1, 3, 1, 0, 2), (4, 0, -1, 5, 0),
-    (1, 2, 0, -1, 2), (1, 2, 0, 1, 2), (1, 2, 1, 2, -1), (1, 2, 1, 2, 1), (3, 3, 0, 0, 0), (4, 1, 1, 4, 0), (4, 0, 1, 5, 0),
-    (1, 2, 0, 2, -1), (1, 2, 0, 2, 1), (1, 2, 1, -1, 2), (1, 2, 1, 1, 2), (3, 2, -1, 0, 0), (4, 1, 2, 3, 0),
-    (4, 1, -1, 5, 0), (1, 3, 0, -1, 2), (1, 3, 1, 2, -1), (4, 0, 2, 4, 0), (1, 3, 1, 2, 1), (1, 3, 0, 2, -1),
-    (3, 2, 1, 0, 0), (4, 2, 0, 3, 0), (4, 3, 0, 2, 0), (1, 3, 0, 1, 2), (1, 3, 0, 2, 1), (1, 3, 1, 1, 2), (1, 3, 1, -1, 2),
-    (3, 3, -1, 0, 0), (4, 1, 1, 5, 0), (4, 2, -1, 2, 0), (1, 2, 0, 2, 2), (1, 2, 1, 2, 2), (3, 3, 1, 0, 0), (4, 1, 2, 4, 0),
-    (1, 3, 1, 2, 2), (4, 2, 1, 2, 0), (4, 0, 2, 5, 0), (1, 3, 0, 2, 2), (3, 2, 2, 0, 0), (4, 2, 0, 4, 0), (3, 3, 2, 0, 0),
-    (4, 3, -1, 2, 0), (4, 3, 0, 3, 0), (4, 2, -1, 3, 0), (4, 3, 1, 2, 0), (4, 1, 2, 5, 0), (4, 2, 2, 2, 0), (4, 2, 1, 3, 0),
-    (4, 2, 0, 5, 0), (4, 3, 2, 2, 0), (4, 3, -1, 3, 0), (4, 3, 0, 4, 0), (4, 2, -1, 4, 0), (4, 3, 1, 3, 0), (4, 2, 2, 3, 0),
-    (4, 2, 1, 4, 0), (4, 3, 2, 3, 0), (4, 3, -1, 4, 0), (4, 3, 0, 5, 0), (4, 2, -1, 5, 0), (4, 3, 1, 4, 0), (4, 2, 2, 4, 0),
-    (4, 2, 1, 5, 0), (4, 3, 2, 4, 0), (4, 3, -1, 5, 0), (4, 3, 1, 5, 0), (4, 2, 2, 5, 0), (4, 3, 2, 5, 0),
+    (1, 0, 0, -1, 2), (1, 0, 0, 1, 2), (1, 0, 1, 2, -1), (1, 0, 1, 2, 1), (3, 1, 0, 0, 0), (4, 0, 0, 2, 0), (0, 2, 0, 0, 0),
+    (1, 0, 0, 2, -1), (1, 0, 0, 2, 1), (1, 0, 1, -1, 2), (1, 0, 1, 1, 2), (3, 0, -1, 0, 0), (1, 1, 0, -1, 2),
+    (1, 1, 1, 2, -1), (1, 1, 0, 2, -1), (1, 1, 1, -1, 2), (3, 0, 1, 0, 0), (1, 1, 0, 1, 2), (1, 1, 0, 2, 1),
+    (1, 1, 1, 1, 2), (1, 1, 1, 2, 1), (3, 1, -1, 0, 0), (4, 1, 0, 2, 0), (0, 3, 0, 0, 0), (1, 0, 1, 2, 2), (1, 2, 1, -1, 0),
+    (1, 2, 1, 1, 0), (1, 2, 0, -1, 0), (3, 1, 1, 0, 0), (4, 0, 0, 3, 0), (4, 0, -1, 2, 0), (1, 2, 0, 0, -1),
+    (1, 2, 0, 0, 1), (1, 2, 1, 0, -1), (1, 2, 0, 1, 0), (4, 0, 1, 2, 0), (1, 1, 0, 2, 2), (1, 0, 0, 2, 2), (1, 1, 1, 2, 2),
+    (1, 2, 1, 0, 1), (4, 1, -1, 2, 0), (1, 3, 1, -1, 0), (1, 3, 1, 1, 0), (1, 3, 0, -1, 0), (1, 3, 0, 1, 0),
+    (3, 0, 2, 0, 0), (4, 1, 0, 3, 0), (4, 1, 1, 2, 0), (1, 3, 0, 0, -1), (1, 3, 0, 0, 1), (1, 3, 1, 0, -1), (1, 3, 1, 0, 1),
+    (3, 1, 2, 0, 0), (4, 0, 0, 4, 0), (1, 2, 1, 2, 0), (1, 2, 0, -1, -1), (4, 0, -1, 3, 0), (1, 2, 1, -1, -1),
+    (1, 2, 1, -1, 1), (4, 0, 1, 3, 0), (1, 2, 0, 0, 2), (1, 2, 0, -1, 1), (1, 2, 1, 1, -1), (1, 2, 1, 1, 1),
+    (4, 1, -1, 3, 0), (4, 0, 2, 2, 0), (1, 2, 0, 1, -1), (1, 2, 0, 1, 1), (1, 2, 0, 2, 0), (1, 3, 1, -1, 1),
+    (3, 2, 0, 0, 0), (4, 1, 0, 4, 0), (1, 2, 1, 0, 2), (1, 3, 1, 2, 0), (1, 3, 0, -1, 1), (1, 3, 1, 1, 1), (4, 1, 1, 3, 0),
+    (4, 1, 2, 2, 0), (4, 0, 0, 5, 0), (1, 3, 0, -1, -1), (1, 3, 0, 1, 1), (1, 3, 1, -1, -1), (1, 3, 0, 2, 0),
+    (4, 0, -1, 4, 0), (4, 0, 1, 4, 0), (1, 3, 0, 0, 2), (1, 3, 0, 1, -1), (1, 3, 1, 1, -1), (1, 3, 1, 0, 2),
+    (4, 1, -1, 4, 0), (4, 2, 0, 2, 0), (4, 0, 2, 3, 0), (1, 2, 0, -1, 2), (1, 2, 0, 1, 2), (1, 2, 1, 2, -1),
+    (1, 2, 1, 2, 1), (3, 3, 0, 0, 0), (4, 1, 0, 5, 0), (1, 2, 0, 2, -1), (1, 2, 0, 2, 1), (4, 1, 1, 4, 0), (1, 2, 1, -1, 2),
+    (1, 2, 1, 1, 2), (3, 2, -1, 0, 0), (4, 1, 2, 3, 0), (4, 0, -1, 5, 0), (1, 3, 0, -1, 2), (1, 3, 1, 2, -1),
+    (1, 3, 0, 2, -1), (1, 3, 1, -1, 2), (3, 2, 1, 0, 0), (4, 0, 1, 5, 0), (4, 1, -1, 5, 0), (1, 3, 0, 1, 2),
+    (1, 3, 1, 2, 1), (1, 3, 0, 2, 1), (1, 3, 1, 1, 2), (3, 3, -1, 0, 0), (4, 2, 0, 3, 0), (4, 3, 0, 2, 0), (4, 0, 2, 4, 0),
+    (1, 2, 0, 2, 2), (1, 2, 1, 2, 2), (3, 3, 1, 0, 0), (4, 1, 1, 5, 0), (4, 2, -1, 2, 0), (1, 3, 1, 2, 2), (1, 3, 0, 2, 2),
+    (3, 2, 2, 0, 0), (4, 1, 2, 4, 0), (4, 2, 1, 2, 0), (3, 3, 2, 0, 0), (4, 3, -1, 2, 0), (4, 2, 0, 4, 0), (4, 3, 0, 3, 0),
+    (4, 3, 1, 2, 0), (4, 0, 2, 5, 0), (4, 2, 2, 2, 0), (4, 2, -1, 3, 0), (4, 1, 2, 5, 0), (4, 3, 2, 2, 0), (4, 2, 1, 3, 0),
+    (4, 3, -1, 3, 0), (4, 2, 0, 5, 0), (4, 3, 0, 4, 0), (4, 3, 1, 3, 0), (4, 2, 2, 3, 0), (4, 2, -1, 4, 0), (4, 3, 2, 3, 0),
+    (4, 2, 1, 4, 0), (4, 3, -1, 4, 0), (4, 3, 0, 5, 0), (4, 3, 1, 4, 0), (4, 2, 2, 4, 0), (4, 2, -1, 5, 0), (4, 3, 2, 4, 0),
+    (4, 2, 1, 5, 0), (4, 3, -1, 5, 0), (4, 3, 1, 5, 0), (4, 2, 2, 5, 0), (4, 3, 2, 5, 0),
 )
 
 

time: 84.9 us -> 84.6 us (level)
  no operation moved by 1% of the time
where the time goes in v4:
time: 84.6 us; the launch traced here: 84 us
  Pallas kernels  82 us (97%)
  local copies, waits for them, and re-layouts  2.04 us (2%)
    pallas_call x1, Pallas kernels, body(): pl.pallas_call(functools.partial(kernel, (rows, depth, own, planes)), out...  82 us
    transpose x1, local copies, waits for them, and re-layouts, body(): return summed.T  2.04 us

profile of v4, /device:TPU:32, one launch (start us, length us, event | category | flops | bytes accessed | tf_op | source)
XLA Modules:
  0.0 84.0 jit_solution(14750517863331485636)
XLA Ops:
  0.0 82.0 %shard_map.37 = f32[256,512]{1,0:T(8,128)} custom-call(s32[8]{0:T(128)} %units_ref.1, f32[512,2048]{1,0:T(8,128)} %v_hbm.1, f32[64,2048]{1,0:T(8,128)} %bitcast.3), custom_call_target="tpu_custom_call" | custom-call | flops 12884901888 | bytes 4194304 | tf_op jit(solution)/shard_map/pallas_call | solution.py:306
  82.0 2.0 %copy.4 = f32[512,256]{1,0:T(8,128)} copy(f32[512,256]{0,1:T(8,128)} %bitcast.2) | data formatting | bytes 1048576 | tf_op jit(solution)/shard_map/transpose | solution.py:338
